TPU v7x, 32 devices: a whole 2x2x4 slice. The times are simulated.
32 devices in a mesh: grp: 1, mid: 16 (over z, y, core), off: 2 (over x), sub: 1.
Axes of the slice: x: 2, y: 2, z: 4, core: 2. Of those that a mesh axis runs over, the one named last changes fastest.
Arguments:
- traces: bfloat16 [2, 1024, 1024], P('off', ('grp', 'mid'), 'sub'), may hold values from -6 to 6
- centre_offset: int32 [256], P(('grp', 'mid')), may hold values from 0 to 63
- foot_start: int32 [256, 16], P('grp'), may hold values from 0 to 240
- beam_count: int32 [16], P('grp'), may hold values from 2 to 16, as said below
- operator: bfloat16 [1024, 65536], P('sub', 'mid'), may hold values from -0.1875 to 0.1875
Outputs:
- image: float32 [256, 256], P(('grp', 'mid'))
Inputs may be any that keep to these rules, and one draw needn't show every extreme that they name: `beam_count`: the live beams of all tiles sum to exactly 128, and the largest count is exactly 16.
All inputs are finite; a program needn't handle non-finite values.
Results may differ from a plain program's by a relative error of at most 0.0028.
Values may be sent and summed in bfloat16 or wider, within the bound.
No kernel may reach another device: no remote copies, remote signals or barrier semaphores. Data moves between devices by JAX's collectives and lax.ppermute only.
A program may use at most 64 MiB of HBM per device.

v0:
```python
import math
import jax
import jax.numpy as jnp
from jax import lax
from jax.sharding import PartitionSpec as P

NT = 1024
P_SIZE = 16
FL = 16
DEPTH = 256
HALF = 16
CB_DEV = 16


def padded_2(cells, sides, width):
    for axis, dim in sides:
        count = lax.axis_size(axis)
        ends = count - 1
        head = lax.slice_in_dim(cells, 0, width, axis=dim)
        tail = lax.slice_in_dim(cells, cells.shape[dim] - width, cells.shape[dim], axis=dim)
        cells = jnp.concatenate(
            [
                lax.ppermute(tail, axis, [(i, (i + 1) % count) for i in range(ends)]),
                cells,
                lax.ppermute(head, axis, [((i + 1) % count, i) for i in range(ends)]),
            ],
            axis=dim,
        )
    return cells


def dft_rows(first_row, row_count, freq_block):
    sample_index = first_row + jnp.arange(row_count, dtype=jnp.int32)[:, None]
    column = jnp.arange(NT, dtype=jnp.int32)[None, :]
    within = column % (2 * freq_block)
    frequency = column // (2 * freq_block) * freq_block + within % freq_block
    phase_angle = 2.0 * math.pi / NT * (sample_index * frequency % NT).astype(jnp.float32)
    values = jnp.where(within // freq_block == 1, -jnp.sin(phase_angle), jnp.cos(phase_angle))
    return values / math.sqrt(NT)


def slant_weights(frequency):
    offsets = jnp.arange(-HALF, HALF + 1, dtype=jnp.int32).astype(jnp.float32)
    taper = jnp.exp(-0.5 * (1.5 * offsets / HALF) ** 2)
    taper = taper / jnp.sqrt(jnp.sum(taper * taper))
    slopes = 0.25 * (jnp.arange(P_SIZE, dtype=jnp.int32).astype(jnp.float32) - 0.5 * (P_SIZE - 1))
    theta = (
        2.0
        * math.pi
        / NT
        * slopes[:, None, None]
        * offsets[None, :, None]
        * frequency.astype(jnp.float32)[None, None, :]
    )
    return (taper[None, :, None] * jnp.cos(theta), taper[None, :, None] * jnp.sin(theta))


def form_beams(windows_real, windows_imag, cos_weight, sin_weight):
    high = lax.Precision.HIGHEST
    beam_real = jnp.einsum("pxf,bxf->bpf", cos_weight, windows_real, precision=high) + jnp.einsum(
        "pxf,bxf->bpf", sin_weight, windows_imag, precision=high
    )
    beam_imag = jnp.einsum("pxf,bxf->bpf", cos_weight, windows_imag, precision=high) - jnp.einsum(
        "pxf,bxf->bpf", sin_weight, windows_real, precision=high
    )
    return (beam_real, beam_imag)


def live_rows(beam_count, per_tile, live_total):
    tile_ends = jnp.cumsum(beam_count)
    position = jnp.arange(live_total, dtype=jnp.int32)
    owner = jnp.sum((position[:, None] >= tile_ends[None, :]).astype(jnp.int32), axis=1)
    first = tile_ends - beam_count
    match = owner[:, None] == jnp.arange(beam_count.shape[0], dtype=jnp.int32)[None, :]
    chosen = jnp.sum(jnp.where(match, first[None, :], 0), axis=1)
    return owner * per_tile + position - chosen


def spread_slopes(beams, mid_count):
    return jnp.repeat(beams, mid_count // P_SIZE, axis=1)[:, :, None, :]


def shards(traces, centre_offset, foot_start, beam_count, operator):
    high = lax.Precision.HIGHEST
    mid_count = lax.axis_size("mid")
    mid_index = lax.axis_index("mid")
    sub_index = lax.axis_index("sub")
    samples = traces.shape[2]
    freq_block = samples // 2
    dft_table = dft_rows(sub_index * samples, samples, freq_block)
    partial_value = jnp.dot(traces[0].astype(jnp.float32), dft_table, precision=high)
    spectrum = lax.psum_scatter(partial_value, "sub", scatter_dimension=1, tiled=True)
    padded = padded_2(spectrum, (("mid", 0),), HALF)
    window_index = centre_offset[:, None] + jnp.arange(2 * HALF + 1, dtype=jnp.int32)[None, :]
    windows = padded[window_index]
    frequency = sub_index * freq_block + jnp.arange(freq_block, dtype=jnp.int32)
    cos_weight, sin_weight = slant_weights(frequency)
    beam_real, beam_imag = form_beams(
        windows[:, :, :freq_block], windows[:, :, freq_block:], cos_weight, sin_weight
    )
    live_here = lax.dynamic_index_in_dim(beam_count, mid_index, 0, keepdims=False)
    alive = jnp.arange(CB_DEV, dtype=jnp.int32) < live_here
    beams = jnp.where(
        alive[:, None, None], jnp.concatenate([beam_real, beam_imag], axis=2), 0.0
    ).astype(jnp.bfloat16)
    columns = operator.shape[1]
    slope_count = max(1, P_SIZE // mid_count)
    footprint_size = FL * DEPTH
    first_column = mid_index * columns
    slope_first = first_column // footprint_size
    lateral_first = first_column % footprint_size // DEPTH
    lateral_count = columns // (slope_count * DEPTH)
    starts = lax.dynamic_slice_in_dim(foot_start, slope_first, slope_count, 1)
    kernels = operator.reshape(samples, slope_count, lateral_count * DEPTH)
    outgoing = spread_slopes(beams, mid_count)
    received = lax.all_to_all(outgoing, "mid", split_axis=1, concat_axis=0, tiled=True)
    row_total = received.shape[0]
    received = received.reshape(row_total, slope_count, samples)
    chosen = live_rows(beam_count, CB_DEV, row_total // 2)
    received = received[chosen]
    starts = starts[chosen]
    centres_all = CB_DEV * mid_count
    block_rows = received.shape[0] // 8
    lateral_steps = lateral_first + jnp.arange(lateral_count, dtype=jnp.int32)
    weight_scale = 1.0 / math.sqrt(FL * P_SIZE)

    def add_block(block, partial_image):
        block_beams = lax.dynamic_slice_in_dim(received, block * block_rows, block_rows, 0)
        block_starts = lax.dynamic_slice_in_dim(starts, block * block_rows, block_rows, 0)
        footprint = (
            jnp.einsum(
                "rsk,ksc->rsc",
                block_beams,
                kernels,
                preferred_element_type=jnp.float32,
                precision=None,
            )
            * weight_scale
        )
        target = (block_starts[:, :, None] + lateral_steps[None, None, :]).reshape(-1)
        return partial_image.at[target].add(footprint.reshape(-1, DEPTH))

    partial_image = lax.fori_loop(0, 8, add_block, jnp.zeros((centres_all, DEPTH), jnp.float32))
    tile_part = lax.psum_scatter(partial_image, "mid", scatter_dimension=0, tiled=True)
    image_tile = lax.psum(tile_part, ("off", "sub"))
    return image_tile


def solution(mesh):
    return jax.shard_map(
        shards,
        mesh=mesh,
        in_specs=(
            P("off", ("grp", "mid"), "sub"),
            P(("grp", "mid")),
            P("grp", None),
            P("grp"),
            P("sub", "mid"),
        ),
        out_specs=P(("grp", "mid"), None),
        check_vma=False,
    )
```

profile of v0, /device:TPU:0, one launch (start us, length us, event | category | flops | bytes accessed | tf_op | source)
XLA Modules:
  0.0 302.9 jit_solution(10258780660640773657)
XLA Ops:
  6.6 0.9 copy-done
  7.4 19.2 %fusion.60 = f32[64,1024]{1,0:T(8,128)S(1)} fusion(s32[1024]{0:T(1024)S(1)} %fusion.67, pred[1024]{0:T(1024)(128)(4,1)S(1)} %fusion.64, bf16[1,64,1024]{2,1,0:T(8,128)(2,1)S(1)} %copy-done), kind=kOutput, calls=%fused_computation.61 | convolution fusion | flops 823132160 | bytes 398336 | tf_op jit(solution)/shard_map/dot_general | solution.py:91
  26.7 2.4 collective-permute-start
  29.1 1.5 collective-permute-start.1
  30.6 0.6 multiply_reduce_fusion
  32.2 0.6 dynamic_slice.24
  32.8 0.6 iota_compare_fusion.2
  33.4 0.9 collective-permute-done.1
  34.4 2.5 gather_fusion.1
  36.8 1.7 reshape.394
  38.5 2.0 fusion.81
  40.5 3.7 %copy.23 = f32[16,33,512]{1,0,2:T(8,128)} copy(f32[16,33,512]{2,1,0:T(8,128)S(1)} %get-tuple-element.148) | data formatting | bytes 2162688
  44.2 3.8 %copy.24 = f32[16,33,512]{1,0,2:T(8,128)} copy(f32[16,33,512]{2,1,0:T(8,128)S(1)} %get-tuple-element.149) | data formatting | bytes 2162688
  48.0 24.9 %fusion.16 = f32[512,16,16]{2,1,0:T(8,128)S(1)} fusion(f32[16,33,512]{1,0,2:T(8,128)} %copy.23, f32[512]{0:T(512)S(1)} %iota_convert_fusion, f32[16,33]{1,0:T(8,128)S(1)} %broadcast_multiply_fusion, f32[33]{0:T(128)S(1)} %broadcast_divide_fusion), kind=kOutput, calls=%fused_computation.24 | convolution fusion | flops 52445184 | bytes 1609924 | tf_op jit(solution)/shard_map/pxf,bxf->bpf/dot_general | solution.py:60
  72.9 22.2 %fusion.14 = f32[512,16,16]{2,1,0:T(8,128)S(1)} fusion(f32[16,33,512]{1,0,2:T(8,128)S(1)} %copy-done.3, f32[512]{0:T(512)S(1)} %iota_convert_fusion, f32[16,33]{1,0:T(8,128)S(1)} %broadcast_multiply_fusion, f32[33]{0:T(128)S(1)} %broadcast_divide_fusion), kind=kOutput, calls=%fused_computation.23 | convolution fusion | flops 52445184 | bytes 1609924 | tf_op jit(solution)/shard_map/pxf,bxf->bpf/dot_general | solution.py:63
  95.1 23.7 %add_bitcast_fusion = bf16[16,16,1,512]{1,0,3,2:T(8,128)(2,1)S(1)} fusion(f32[512,16,16]{2,1,0:T(8,128)S(1)} %fusion.16, f32[16,33,512]{1,0,2:T(8,128)S(1)} %copy-done.3, f32[512]{0:T(512)S(1)} %iota_convert_fusion, f32[16,33]{1,0:T(8,128)S(1)} %broadcast_multiply_fusion, f32[33]{0:T(128)S(1)} %broadcast_divide_fusion), kind=kOutput, calls=%fused_computation.32 | convolution fusion | flops 52707328 | bytes 1872068 | tf_op jit(solution)/shard_map/pxf,bxf->bpf/dot_general | solution.py:60
  118.9 23.7 %subtract_bitcast_fusion = bf16[16,16,1,512]{1,0,3,2:T(8,128)(2,1)S(1)} fusion(f32[512,16,16]{2,1,0:T(8,128)S(1)} %fusion.14, f32[16,33,512]{1,0,2:T(8,128)S(1)} %copy-done.2, f32[512]{0:T(512)S(1)} %iota_convert_fusion, f32[16,33]{1,0:T(8,128)S(1)} %broadcast_multiply_fusion, f32[33]{0:T(128)S(1)} %broadcast_divide_fusion), kind=kOutput, calls=%fused_computation.31 | convolution fusion | flops 52707328 | bytes 1872068 | tf_op jit(solution)/shard_map/pxf,bxf->bpf/dot_general | solution.py:63
  142.6 2.6 maximum_select_fusion
  145.2 5.7 %copy.22 = bf16[16,16,1,1024]{3,0,2,1:T(8,128)(2,1)} copy(bf16[16,16,1,1024]{1,0,3,2:T(8,128)(2,1)} %maximum_select_fusion) | data formatting | bytes 1048576 | tf_op jit(solution)/shard_map/jit(_where)/select_n | solution.py:103
  150.8 8.4 %all-to-all-start = ((bf16[16,16,1,1024]{3,0,2,1:T(8,128)(2,1)}), bf16[16,16,1,1024]{3,0,2,1:T(8,128)(2,1)S(1)}, u32[]{:S(2)}, u32[]{:S(2)}) async-start(bf16[16,16,1,1024]{3,0,2,1:T(8,128)(2,1)} %copy.22), calls=%async_computation | async-start | bytes 1048576 | tf_op jit(solution)/shard_map/all_to_all | solution.py:116
  159.2 0.3 reduce-scatter.2.cloned.1.call-start
  159.7 0.1 reduce.1
  159.8 0.7 constant_dynamic-slice_fusion
  160.7 1.3 gather_fusion
  162.0 11.5 %all-to-all-done = bf16[16,16,1,1024]{3,0,2,1:T(8,128)(2,1)S(1)} async-done(((bf16[16,16,1,1024]{3,0,2,1:T(8,128)(2,1)}), bf16[16,16,1,1024]{3,0,2,1:T(8,128)(2,1)S(1)}, u32[]{:S(2)}, u32[]{:S(2)}) %all-to-all-start) | async-done | bytes 524320 | tf_op jit(solution)/shard_map/all_to_all | solution.py:116
  173.5 0.9 gather_fusion.2
  174.4 56.2 %while.14 = (s32[]{:T(128)}, f32[256,256]{1,0:T(8,128)S(1)}, s32[128,1]{0,1:T(1,128)S(1)}, bf16[128,1,1024]{2,0,1:T(8,128)(2,1)S(1)}, bf16[1024,1,4096]{2,0,1:T(...) while((s32[]{:T(128)}, f32[256,256]{1,0:T(8,128)S(1)}, ...), condition=%wide.region_6.7_spmd.clone, body=%wide.region_4.6_spmd.clone.sunk | while | flops 134349840 | bytes 10000863 | solution.py:143
  174.4 4.6 %fusion.92 = f32[16,1,4096]{2,0,1:T(8,128)S(1)} fusion(bf16[1024,1,4096]{2,0,1:T(8,128)(2,1)} %get-tuple-element.213, bf16[128,1,1024]{2,0,1:T(8,128)(2,1)S(1)} %get-tuple-element.212, s32[]{:T(128)S(6)} %select_n.211), kind=kOutput, calls=%fused_computation.8.clone.1 | convolution fusion | flops 134283264 | bytes 8683524 | tf_op jit(solution)/shard_map/while/body/eval_jaxpr/rsk,ksc->rsc/dot_general | solution.py:131
  179.1 0.1 add_reduce_fusion.2
  179.3 2.1 scatter_fusion
  181.4 4.6 %fusion.92 = f32[16,1,4096]{2,0,1:T(8,128)S(1)} fusion(bf16[1024,1,4096]{2,0,1:T(8,128)(2,1)} %get-tuple-element.213, bf16[128,1,1024]{2,0,1:T(8,128)(2,1)S(1)} %get-tuple-element.212, s32[]{:T(128)S(6)} %select_n.211), kind=kOutput, calls=%fused_computation.8.clone.1 | convolution fusion | flops 134283264 | bytes 8683524 | tf_op jit(solution)/shard_map/while/body/eval_jaxpr/rsk,ksc->rsc/dot_general | solution.py:131
  186.1 0.1 add_reduce_fusion.2
  186.3 2.1 scatter_fusion
  188.4 4.6 %fusion.92 = f32[16,1,4096]{2,0,1:T(8,128)S(1)} fusion(bf16[1024,1,4096]{2,0,1:T(8,128)(2,1)} %get-tuple-element.213, bf16[128,1,1024]{2,0,1:T(8,128)(2,1)S(1)} %get-tuple-element.212, s32[]{:T(128)S(6)} %select_n.211), kind=kOutput, calls=%fused_computation.8.clone.1 | convolution fusion | flops 134283264 | bytes 8683524 | tf_op jit(solution)/shard_map/while/body/eval_jaxpr/rsk,ksc->rsc/dot_general | solution.py:131
  193.3 2.1 scatter_fusion
  195.5 4.6 %fusion.92 = f32[16,1,4096]{2,0,1:T(8,128)S(1)} fusion(bf16[1024,1,4096]{2,0,1:T(8,128)(2,1)} %get-tuple-element.213, bf16[128,1,1024]{2,0,1:T(8,128)(2,1)S(1)} %get-tuple-element.212, s32[]{:T(128)S(6)} %select_n.211), kind=kOutput, calls=%fused_computation.8.clone.1 | convolution fusion | flops 134283264 | bytes 8683524 | tf_op jit(solution)/shard_map/while/body/eval_jaxpr/rsk,ksc->rsc/dot_general | solution.py:131
  200.4 2.1 scatter_fusion
  202.5 4.6 %fusion.92 = f32[16,1,4096]{2,0,1:T(8,128)S(1)} fusion(bf16[1024,1,4096]{2,0,1:T(8,128)(2,1)} %get-tuple-element.213, bf16[128,1,1024]{2,0,1:T(8,128)(2,1)S(1)} %get-tuple-element.212, s32[]{:T(128)S(6)} %select_n.211), kind=kOutput, calls=%fused_computation.8.clone.1 | convolution fusion | flops 134283264 | bytes 8683524 | tf_op jit(solution)/shard_map/while/body/eval_jaxpr/rsk,ksc->rsc/dot_general | solution.py:131
  207.4 2.1 scatter_fusion
  209.5 4.6 %fusion.92 = f32[16,1,4096]{2,0,1:T(8,128)S(1)} fusion(bf16[1024,1,4096]{2,0,1:T(8,128)(2,1)} %get-tuple-element.213, bf16[128,1,1024]{2,0,1:T(8,128)(2,1)S(1)} %get-tuple-element.212, s32[]{:T(128)S(6)} %select_n.211), kind=kOutput, calls=%fused_computation.8.clone.1 | convolution fusion | flops 134283264 | bytes 8683524 | tf_op jit(solution)/shard_map/while/body/eval_jaxpr/rsk,ksc->rsc/dot_general | solution.py:131
  214.4 2.1 scatter_fusion
  216.5 4.6 %fusion.92 = f32[16,1,4096]{2,0,1:T(8,128)S(1)} fusion(bf16[1024,1,4096]{2,0,1:T(8,128)(2,1)} %get-tuple-element.213, bf16[128,1,1024]{2,0,1:T(8,128)(2,1)S(1)} %get-tuple-element.212, s32[]{:T(128)S(6)} %select_n.211), kind=kOutput, calls=%fused_computation.8.clone.1 | convolution fusion | flops 134283264 | bytes 8683524 | tf_op jit(solution)/shard_map/while/body/eval_jaxpr/rsk,ksc->rsc/dot_general | solution.py:131
  221.4 2.1 scatter_fusion
  223.5 4.6 %fusion.92 = f32[16,1,4096]{2,0,1:T(8,128)S(1)} fusion(bf16[1024,1,4096]{2,0,1:T(8,128)(2,1)} %get-tuple-element.213, bf16[128,1,1024]{2,0,1:T(8,128)(2,1)S(1)} %get-tuple-element.212, s32[]{:T(128)S(6)} %select_n.211), kind=kOutput, calls=%fused_computation.8.clone.1 | convolution fusion | flops 134283264 | bytes 8683524 | tf_op jit(solution)/shard_map/while/body/eval_jaxpr/rsk,ksc->rsc/dot_general | solution.py:131
  228.4 2.1 scatter_fusion
  230.5 0.7 copy-done.1
  231.3 55.4 %reduce-scatter.2.cloned.1.call-done = f32[16,256]{1,0:T(8,128)} async-done(((f32[256,256]{1,0:T(8,128)}), f32[16,256]{1,0:T(8,128)}) %reduce-scatter.2.cloned.1.call-update) | async-done | bytes 16400 | tf_op jit(solution)/shard_map/reduce_scatter | solution.py:144
  286.7 9.4 %psum.7 = f32[16,256]{1,0:T(8,128)} all-reduce(f32[16,256]{1,0:T(8,128)} %reduce-scatter.2.cloned.1.call-done), channel_id=1, replica_groups=mesh['grp'=1,'mid'=16,'off'=2,'sub'=1] {'off','sub'}, use_global_device_ids=true, to_apply=%region_8.9 | all-reduce | flops 4096 | bytes 32768 | tf_op jit(solution)/shard_map/psum | solution.py:145
  (78 shorter events, 3.0 us)
Async XLA Ops:
  6.5 0.9 copy-start
  7.4 23.8 %copy-start.4 = (s32[16]{0:T(128)S(1)}, s32[16]{0:T(128)}, u32[]{:S(2)}) copy-start(s32[16]{0:T(128)} %param.8) | copy-start | bytes 196
  7.4 24.7 %copy-start.5 = (s32[16]{0:T(128)S(1)}, s32[16]{0:T(128)}, u32[]{:S(2)}) copy-start(s32[16]{0:T(128)} %param.10) | copy-start | bytes 196
  26.7 6.7 %collective-permute-start = (f32[16,1024]{1,0:T(8,128)S(1)}, f32[16,1024]{1,0:T(8,128)S(1)}, u32[]{:S(2)}, u32[]{:S(2)}) collective-permute-start(f32[16,1024]{1,0:T(8,128)S(1)} %get-tuple-element.150), channel_id=1, source_target_pairs={{0,2},{2,4},{4,6},{6,8},{8,10},{10,12},{12,14},{14,16},{16,18},{18... | collective-permute-start | bytes 196616 | tf_op jit(solution)/shard_map/ppermute | solution.py:23
  29.1 5.3 %collective-permute-start.1 = (f32[16,1024]{1,0:T(8,128)S(1)}, f32[16,1024]{1,0:T(8,128)S(1)}, u32[]{:S(2)}, u32[]{:S(2)}) collective-permute-start(f32[16,1024]{1,0:T(8,128)S(1)} %get-tuple-element.151), channel_id=1, source_target_pairs={{2,0},{4,2},{6,4},{8,6},{10,8},{12,10},{14,12},{16,14},{18,16},{20... | collective-permute-start | bytes 196616 | tf_op jit(solution)/shard_map/ppermute | solution.py:25
  48.0 24.9 %copy-start.3 = (f32[16,33,512]{1,0,2:T(8,128)S(1)}, f32[16,33,512]{1,0,2:T(8,128)}, u32[]{:S(2)}) copy-start(f32[16,33,512]{1,0,2:T(8,128)} %copy.24) | copy-start | bytes 3244036
  95.1 23.8 %copy-start.2 = (f32[16,33,512]{1,0,2:T(8,128)S(1)}, f32[16,33,512]{1,0,2:T(8,128)}, u32[]{:S(2)}) copy-start(f32[16,33,512]{1,0,2:T(8,128)} %copy.23) | copy-start | bytes 3244036
  150.8 22.7 %all-to-all-start = ((bf16[16,16,1,1024]{3,0,2,1:T(8,128)(2,1)}), bf16[16,16,1,1024]{3,0,2,1:T(8,128)(2,1)S(1)}, u32[]{:S(2)}, u32[]{:S(2)}) async-start(bf16[16,16,1,1024]{3,0,2,1:T(8,128)(2,1)} %copy.22), calls=%async_computation | async-start | bytes 1048576 | tf_op jit(solution)/shard_map/all_to_all | solution.py:116
  159.2 127.5 %reduce-scatter.2.cloned.1.call-start = ((), (), s32[]{:S(2)}) async-start(), calls=%async_computation.2 | async-start | bytes 278528 | tf_op jit(solution)/shard_map/reduce_scatter | solution.py:144
  230.5 0.7 copy-start.1
Sparse Core Ops, SparseCore 0:
  231.4 55.2 reduce-scatter.1
where the time goes:
time: 304 us; the launch traced here: 303 us
  matrix products  150 us (49%)
  waiting for transfers between devices  67.9 us (22%)
  local copies, waits for them, and re-layouts  26.1 us (9%)
  other arithmetic  21.8 us (7%)
  between operations  14.4 us (5%)
  starting transfers between devices  12.5 us (4%)
  blocking collectives  9.37 us (3%)
    reduce_scatter x1, waiting for transfers between devices, shards(): lax.psum_scatter(partial_image, 'mid', scatter_dimension=0, tiled=True)  55.4 us
    dot_general x8, matrix products, add_block(): jnp.einsum('rsk,ksc->rsc', block_beams, kernels, preferred_element_type=j...  36.7 us
    dot_general x1, matrix products, form_beams(): jnp.einsum('pxf,bxf->bpf', cos_weight, windows_real, precision=high)  24.9 us
    dot_general x1, matrix products, form_beams(): jnp.einsum('pxf,bxf->bpf', sin_weight, windows_imag, precision=high)  23.7 us
    dot_general x1, matrix products, form_beams(): jnp.einsum('pxf,bxf->bpf', sin_weight, windows_real, precision=high)  23.7 us
    dot_general x1, matrix products, form_beams(): jnp.einsum('pxf,bxf->bpf', cos_weight, windows_imag, precision=high)  22.2 us
    dot_general x1, matrix products, shards(): jnp.dot(traces[0].astype(jnp.float32), dft_table, precision=high)  19.2 us
    scatter-add x8, other arithmetic, add_block(): return partial_image.at[target].add(footprint.reshape(-1, DEPTH))  16.6 us
  transfers between devices with their start and end apart: 4, of which 3 were waited for; matrix products, arithmetic and copies ran while one was open for 1% of the time, Pallas kernels for 0%

commit v1 on v0

--- a/solution.py
+++ b/solution.py
@@ -1,3 +1,4 @@
+import functools
 import math
 import jax
 import jax.numpy as jnp
@@ -10,6 +11,25 @@
 DEPTH = 256
 HALF = 16
 CB_DEV = 16
+
+
+def get_chunk(my_data, mesh_ax):
+    aux, frame_out = (lax.psum(1, axis_name=mesh_ax), lax.axis_index(mesh_ax))
+    y1 = my_data.shape[1] // aux
+    answer = jnp.roll(my_data, -frame_out * y1, 1)
+    current_arr = lax.slice_in_dim(answer, 0, y1, axis=1)
+    bank = [current_arr]
+    for nth in [*range(1, aux)]:
+        shaped = lax.slice_in_dim(answer, nth * y1, (nth + 1) * y1, axis=1)
+        local_now = lax.ppermute(
+            shaped, mesh_ax, [(tick, (tick + nth) % aux) for tick in range(aux)]
+        )
+        bank.append(local_now)
+    x_new = jnp.concatenate(bank[::-1], 0)
+    return jnp.roll(x_new, (frame_out + 1) * bank[0].shape[0], 0)
+
+
+perform_body = functools.partial(get_chunk, mesh_ax="mid")
 
 
 def padded_2(cells, sides, width):
@@ -113,7 +133,7 @@
     starts = lax.dynamic_slice_in_dim(foot_start, slope_first, slope_count, 1)
     kernels = operator.reshape(samples, slope_count, lateral_count * DEPTH)
     outgoing = spread_slopes(beams, mid_count)
-    received = lax.all_to_all(outgoing, "mid", split_axis=1, concat_axis=0, tiled=True)
+    received = perform_body(outgoing)
     row_total = received.shape[0]
     received = received.reshape(row_total, slope_count, samples)
     chosen = live_rows(beam_count, CB_DEV, row_total // 2)

time: 304 us -> 311 us (1.023)
  starting transfers between devices: 12.5 us -> 28.4 us
  waiting for transfers between devices: 67.9 us -> 59.6 us
    ppermute x0 -> x15, starting transfers between devices: none -> 24.5 us  [get_chunk(): lax.ppermute(shaped, mesh_ax, [(tick, (tick + nth) % aux) for tick in ran...]
    all_to_all x1 -> x0, waiting for transfers between devices: 11.5 us -> none  [shards(): lax.all_to_all(outgoing, 'mid', split_axis=1, concat_axis=0, tiled=True)]
    all_to_all x1 -> x0, starting transfers between devices: 8.38 us -> none  [shards(): lax.all_to_all(outgoing, 'mid', split_axis=1, concat_axis=0, tiled=True)]
    ppermute x0 -> x15, waiting for transfers between devices: none -> 6.01 us  [get_chunk(): lax.ppermute(shaped, mesh_ax, [(tick, (tick + nth) % aux) for tick in ran...]
    select_n x1 -> x0, local copies, waits for them, and re-layouts: 5.67 us -> none  [shards(): jnp.where(alive[:, None, None], jnp.concatenate([beam_real, beam_imag], a...]
    concatenate x0 -> x3, local copies, waits for them, and re-layouts: none -> 3.47 us  [the longest x2 3.46 us: shards(): jnp.concatenate([beam_real, beam_imag], axis=2)]
    unnamed x14 -> x58, local copies, waits for them, and re-layouts: 9.09 us -> 9.45 us
  transfers between devices with their start and end apart: 4 -> 18, of which waited for: 3 -> 6; matrix products, arithmetic and copies ran while one was open for 1% -> 2% of each run, Pallas kernels for 0% -> 0%
where the time goes in v1:
time: 311 us; the launch traced here: 310 us
  matrix products  152 us (49%)
  waiting for transfers between devices  59.6 us (19%)
  starting transfers between devices  28.4 us (9%)
  local copies, waits for them, and re-layouts  25.4 us (8%)
  other arithmetic  19.8 us (6%)
  between operations  14.6 us (5%)
  blocking collectives  9.37 us (3%)
    reduce_scatter x1, waiting for transfers between devices, shards(): lax.psum_scatter(partial_image, 'mid', scatter_dimension=0, tiled=True)  53.1 us
    dot_general x8, matrix products, add_block(): jnp.einsum('rsk,ksc->rsc', block_beams, kernels, preferred_element_type=j...  36.7 us
    dot_general x1, matrix products, form_beams(): jnp.einsum('pxf,bxf->bpf', cos_weight, windows_real, precision=high)  24.9 us
    ppermute x15, starting transfers between devices, get_chunk(): lax.ppermute(shaped, mesh_ax, [(tick, (tick + nth) % aux) for tick in ran...  24.5 us
    dot_general x1, matrix products, form_beams(): jnp.einsum('pxf,bxf->bpf', cos_weight, windows_imag, precision=high)  24.4 us
    dot_general x1, matrix products, form_beams(): jnp.einsum('pxf,bxf->bpf', sin_weight, windows_imag, precision=high)  23.7 us
    dot_general x1, matrix products, form_beams(): jnp.einsum('pxf,bxf->bpf', sin_weight, windows_real, precision=high)  23.6 us
    dot_general x1, matrix products, shards(): jnp.dot(traces[0].astype(jnp.float32), dft_table, precision=high)  19.2 us
  transfers between devices with their start and end apart: 18, of which 6 were waited for; matrix products, arithmetic and copies ran while one was open for 2% of the time, Pallas kernels for 0%

profile of v1, /device:TPU:0, one launch (start us, length us, event | category | flops | bytes accessed | tf_op | source)
XLA Modules:
  0.0 310.0 jit_solution(11967952198505189087)
XLA Ops:
  6.6 0.9 copy-done
  7.4 19.2 %fusion.60 = f32[64,1024]{1,0:T(8,128)S(1)} fusion(s32[1024]{0:T(1024)S(1)} %fusion.69, pred[1024]{0:T(1024)(128)(4,1)S(1)} %fusion.66, bf16[1,64,1024]{2,1,0:T(8,128)(2,1)S(1)} %copy-done), kind=kOutput, calls=%fused_computation.60 | convolution fusion | flops 823132160 | bytes 398336 | tf_op jit(solution)/shard_map/dot_general | solution.py:111
  26.7 2.4 collective-permute-start
  29.1 1.5 collective-permute-start.1
  34.4 2.5 gather_fusion.1
  36.8 1.7 reshape.393
  38.5 2.0 fusion.83
  40.5 3.7 %copy.25 = f32[16,33,512]{1,0,2:T(8,128)} copy(f32[16,33,512]{2,1,0:T(8,128)S(1)} %get-tuple-element.148) | data formatting | bytes 2162688
  44.2 3.8 %copy.26 = f32[16,33,512]{1,0,2:T(8,128)} copy(f32[16,33,512]{2,1,0:T(8,128)S(1)} %get-tuple-element.149) | data formatting | bytes 2162688
  48.0 24.9 %fusion.16 = f32[512,16,16]{2,1,0:T(8,128)S(1)} fusion(f32[16,33,512]{1,0,2:T(8,128)} %copy.25, f32[512]{0:T(512)S(1)} %iota_convert_fusion, f32[16,33]{1,0:T(8,128)S(1)} %broadcast_multiply_fusion, f32[33]{0:T(128)S(1)} %broadcast_divide_fusion), kind=kOutput, calls=%fused_computation.23 | convolution fusion | flops 52445184 | bytes 1609924 | tf_op jit(solution)/shard_map/pxf,bxf->bpf/dot_general | solution.py:80
  72.9 24.4 %fusion.14 = f32[512,16,16]{2,1,0:T(8,128)} fusion(f32[16,33,512]{1,0,2:T(8,128)S(1)} %copy-done.2, f32[512]{0:T(512)S(1)} %iota_convert_fusion, f32[16,33]{1,0:T(8,128)S(1)} %broadcast_multiply_fusion, f32[33]{0:T(128)S(1)} %broadcast_divide_fusion), kind=kOutput, calls=%fused_computation.22 | convolution fusion | flops 52445184 | bytes 1609924 | tf_op jit(solution)/shard_map/pxf,bxf->bpf/dot_general | solution.py:83
  97.3 23.7 %add_bitcast_fusion = bf16[16,16,1,512]{1,0,3,2:T(8,128)(2,1)S(1)} fusion(f32[512,16,16]{2,1,0:T(8,128)S(1)} %fusion.16, f32[16,33,512]{1,0,2:T(8,128)S(1)} %copy-done.2, f32[512]{0:T(512)S(1)} %iota_convert_fusion, f32[16,33]{1,0:T(8,128)S(1)} %broadcast_multiply_fusion, f32[33]{0:T(128)S(1)} %broadcast_divide_fusion), kind=kOutput, calls=%fused_computation.31 | convolution fusion | flops 52707328 | bytes 1872068 | tf_op jit(solution)/shard_map/pxf,bxf->bpf/dot_general | solution.py:80
  121.0 1.6 copy.22
  122.6 23.6 %subtract_bitcast_fusion = bf16[16,16,1,512]{1,0,3,2:T(8,128)(2,1)S(1)} fusion(f32[512,16,16]{2,1,0:T(8,128)} %fusion.14, f32[16,33,512]{1,0,2:T(8,128)} %copy.25, f32[512]{0:T(512)S(1)} %iota_convert_fusion, f32[16,33]{1,0:T(8,128)S(1)} %broadcast_multiply_fusion, f32[33]{0:T(128)S(1)} %broadcast_divide_fusion), kind=kOutput, calls=%fused_computation.30 | convolution fusion | flops 52707328 | bytes 1872068 | tf_op jit(solution)/shard_map/pxf,bxf->bpf/dot_general | solution.py:83
  146.2 1.8 copy.23
  148.6 1.1 fusion.84
  149.7 5.9 %collective-permute-start.2 = (bf16[16,1,1,1024]{3,0,2,1:T(8,128)(2,1)S(1)}, bf16[16,1,1,1024]{3,0,2,1:T(8,128)(2,1)S(1)}, u32[]{:S(2)}, u32[]{:S(2)}) collective-permute-start(bf16[16,1,1,1024]{3,0,2,1:T(8,128)(2,1)S(1)} %copy.28), channel_id=1, source_target_pairs={{0,30},{2,0},{4,2},{6,4},{8,6},{10,8},{12,10},{14,12},{16,14},{18,... | collective-permute-start | bytes 98312 | tf_op jit(solution)/shard_map/ppermute | solution.py:24
  156.4 1.3 gather_fusion
  157.6 1.8 collective-permute-start.3
  161.1 5.0 %collective-permute-start.7 = (bf16[16,1,1,1024]{3,0,2,1:T(8,128)(2,1)S(1)}, bf16[16,1,1,1024]{3,0,2,1:T(8,128)(2,1)S(1)}, u32[]{:S(2)}, u32[]{:S(2)}) collective-permute-start(bf16[16,1,1,1024]{3,0,2,1:T(8,128)(2,1)S(1)} %copy.33), channel_id=1, source_target_pairs={{0,20},{2,22},{4,24},{6,26},{8,28},{10,30},{12,0},{14,2},{16,4},{1... | collective-permute-start | bytes 98312 | tf_op jit(solution)/shard_map/ppermute | solution.py:24
  166.9 1.9 collective-permute-start.10
  168.8 2.0 collective-permute-start.11
  171.1 1.9 collective-permute-start.13
  173.0 2.1 collective-permute-start.14
  175.1 1.5 collective-permute-start.15
  176.8 1.9 collective-permute-done.14
  178.6 3.1 collective-permute-done.15
  181.7 0.9 collective-permute-done.16
  182.9 0.9 gather_fusion.2
  183.8 56.2 %while.14 = (s32[]{:T(128)}, f32[256,256]{1,0:T(8,128)S(1)}, s32[128,1]{0,1:T(1,128)S(1)}, bf16[128,1,1024]{2,0,1:T(8,128)(2,1)S(1)}, bf16[1024,1,4096]{2,0,1:T(...) while((s32[]{:T(128)}, f32[256,256]{1,0:T(8,128)S(1)}, ...), condition=%wide.region_6.7_spmd.clone, body=%wide.region_4.6_spmd.clone.sunk | while | flops 134349840 | bytes 10000863 | solution.py:163
  183.8 4.6 %fusion.95 = f32[16,1,4096]{2,0,1:T(8,128)S(1)} fusion(bf16[1024,1,4096]{2,0,1:T(8,128)(2,1)} %get-tuple-element.229, bf16[128,1,1024]{2,0,1:T(8,128)(2,1)S(1)} %get-tuple-element.228, s32[]{:T(128)S(6)} %select_n.239), kind=kOutput, calls=%fused_computation.8.clone.1 | convolution fusion | flops 134283264 | bytes 8683524 | tf_op jit(solution)/shard_map/while/body/eval_jaxpr/rsk,ksc->rsc/dot_general | solution.py:151
  188.7 2.1 scatter_fusion
  190.8 4.6 %fusion.95 = f32[16,1,4096]{2,0,1:T(8,128)S(1)} fusion(bf16[1024,1,4096]{2,0,1:T(8,128)(2,1)} %get-tuple-element.229, bf16[128,1,1024]{2,0,1:T(8,128)(2,1)S(1)} %get-tuple-element.228, s32[]{:T(128)S(6)} %select_n.239), kind=kOutput, calls=%fused_computation.8.clone.1 | convolution fusion | flops 134283264 | bytes 8683524 | tf_op jit(solution)/shard_map/while/body/eval_jaxpr/rsk,ksc->rsc/dot_general | solution.py:151
  195.7 2.1 scatter_fusion
  197.8 4.6 %fusion.95 = f32[16,1,4096]{2,0,1:T(8,128)S(1)} fusion(bf16[1024,1,4096]{2,0,1:T(8,128)(2,1)} %get-tuple-element.229, bf16[128,1,1024]{2,0,1:T(8,128)(2,1)S(1)} %get-tuple-element.228, s32[]{:T(128)S(6)} %select_n.239), kind=kOutput, calls=%fused_computation.8.clone.1 | convolution fusion | flops 134283264 | bytes 8683524 | tf_op jit(solution)/shard_map/while/body/eval_jaxpr/rsk,ksc->rsc/dot_general | solution.py:151
  202.8 2.1 scatter_fusion
  204.9 4.6 %fusion.95 = f32[16,1,4096]{2,0,1:T(8,128)S(1)} fusion(bf16[1024,1,4096]{2,0,1:T(8,128)(2,1)} %get-tuple-element.229, bf16[128,1,1024]{2,0,1:T(8,128)(2,1)S(1)} %get-tuple-element.228, s32[]{:T(128)S(6)} %select_n.239), kind=kOutput, calls=%fused_computation.8.clone.1 | convolution fusion | flops 134283264 | bytes 8683524 | tf_op jit(solution)/shard_map/while/body/eval_jaxpr/rsk,ksc->rsc/dot_general | solution.py:151
  209.8 2.1 scatter_fusion
  211.9 4.6 %fusion.95 = f32[16,1,4096]{2,0,1:T(8,128)S(1)} fusion(bf16[1024,1,4096]{2,0,1:T(8,128)(2,1)} %get-tuple-element.229, bf16[128,1,1024]{2,0,1:T(8,128)(2,1)S(1)} %get-tuple-element.228, s32[]{:T(128)S(6)} %select_n.239), kind=kOutput, calls=%fused_computation.8.clone.1 | convolution fusion | flops 134283264 | bytes 8683524 | tf_op jit(solution)/shard_map/while/body/eval_jaxpr/rsk,ksc->rsc/dot_general | solution.py:151
  216.8 2.1 scatter_fusion
  218.9 4.6 %fusion.95 = f32[16,1,4096]{2,0,1:T(8,128)S(1)} fusion(bf16[1024,1,4096]{2,0,1:T(8,128)(2,1)} %get-tuple-element.229, bf16[128,1,1024]{2,0,1:T(8,128)(2,1)S(1)} %get-tuple-element.228, s32[]{:T(128)S(6)} %select_n.239), kind=kOutput, calls=%fused_computation.8.clone.1 | convolution fusion | flops 134283264 | bytes 8683524 | tf_op jit(solution)/shard_map/while/body/eval_jaxpr/rsk,ksc->rsc/dot_general | solution.py:151
  223.8 2.1 scatter_fusion
  225.9 4.6 %fusion.95 = f32[16,1,4096]{2,0,1:T(8,128)S(1)} fusion(bf16[1024,1,4096]{2,0,1:T(8,128)(2,1)} %get-tuple-element.229, bf16[128,1,1024]{2,0,1:T(8,128)(2,1)S(1)} %get-tuple-element.228, s32[]{:T(128)S(6)} %select_n.239), kind=kOutput, calls=%fused_computation.8.clone.1 | convolution fusion | flops 134283264 | bytes 8683524 | tf_op jit(solution)/shard_map/while/body/eval_jaxpr/rsk,ksc->rsc/dot_general | solution.py:151
  230.8 2.1 scatter_fusion
  232.9 4.6 %fusion.95 = f32[16,1,4096]{2,0,1:T(8,128)S(1)} fusion(bf16[1024,1,4096]{2,0,1:T(8,128)(2,1)} %get-tuple-element.229, bf16[128,1,1024]{2,0,1:T(8,128)(2,1)S(1)} %get-tuple-element.228, s32[]{:T(128)S(6)} %select_n.239), kind=kOutput, calls=%fused_computation.8.clone.1 | convolution fusion | flops 134283264 | bytes 8683524 | tf_op jit(solution)/shard_map/while/body/eval_jaxpr/rsk,ksc->rsc/dot_general | solution.py:151
  237.9 2.1 scatter_fusion
  240.7 53.1 %reduce-scatter.2.cloned.1.call-done = f32[16,256]{1,0:T(8,128)} async-done(((f32[256,256]{1,0:T(8,128)}), f32[16,256]{1,0:T(8,128)}) %reduce-scatter.2.cloned.1.call-update) | async-done | bytes 16400 | tf_op jit(solution)/shard_map/reduce_scatter | solution.py:164
  293.8 9.4 %psum.7 = f32[16,256]{1,0:T(8,128)} all-reduce(f32[16,256]{1,0:T(8,128)} %reduce-scatter.2.cloned.1.call-done), channel_id=1, replica_groups=mesh['grp'=1,'mid'=16,'off'=2,'sub'=1] {'off','sub'}, use_global_device_ids=true, to_apply=%region_8.9 | all-reduce | flops 4096 | bytes 32768 | tf_op jit(solution)/shard_map/psum | solution.py:165
  (155 shorter events, 10.5 us)
Async XLA Ops:
  6.5 0.9 copy-start
  6.5 287.3 %reduce-scatter.2.cloned.1.call-start = ((), (), s32[]{:S(2)}) async-start(), calls=%async_computation.1 | async-start | bytes 278528 | tf_op jit(solution)/shard_map/reduce_scatter | solution.py:164
  7.4 23.8 %copy-start.4 = (s32[16]{0:T(128)S(1)}, s32[16]{0:T(128)}, u32[]{:S(2)}) copy-start(s32[16]{0:T(128)} %param.10) | copy-start | bytes 196
  7.4 24.2 %copy-start.3 = (s32[16]{0:T(128)S(1)}, s32[16]{0:T(128)}, u32[]{:S(2)}) copy-start(s32[16]{0:T(128)} %param.8) | copy-start | bytes 196
  26.7 7.2 %collective-permute-start = (f32[16,1024]{1,0:T(8,128)S(1)}, f32[16,1024]{1,0:T(8,128)S(1)}, u32[]{:S(2)}, u32[]{:S(2)}) collective-permute-start(f32[16,1024]{1,0:T(8,128)S(1)} %get-tuple-element.166), channel_id=1, source_target_pairs={{0,2},{2,4},{4,6},{6,8},{8,10},{10,12},{12,14},{14,16},{16,18},{18... | collective-permute-start | bytes 196616 | tf_op jit(solution)/shard_map/ppermute | solution.py:43
  29.1 5.3 %collective-permute-start.1 = (f32[16,1024]{1,0:T(8,128)S(1)}, f32[16,1024]{1,0:T(8,128)S(1)}, u32[]{:S(2)}, u32[]{:S(2)}) collective-permute-start(f32[16,1024]{1,0:T(8,128)S(1)} %get-tuple-element.167), channel_id=1, source_target_pairs={{2,0},{4,2},{6,4},{8,6},{10,8},{12,10},{14,12},{16,14},{18,16},{20... | collective-permute-start | bytes 196616 | tf_op jit(solution)/shard_map/ppermute | solution.py:45
  48.0 24.9 %copy-start.2 = (f32[16,33,512]{1,0,2:T(8,128)S(1)}, f32[16,33,512]{1,0,2:T(8,128)}, u32[]{:S(2)}) copy-start(f32[16,33,512]{1,0,2:T(8,128)} %copy.26) | copy-start | bytes 3244036
  149.7 11.3 %collective-permute-start.2 = (bf16[16,1,1,1024]{3,0,2,1:T(8,128)(2,1)S(1)}, bf16[16,1,1,1024]{3,0,2,1:T(8,128)(2,1)S(1)}, u32[]{:S(2)}, u32[]{:S(2)}) collective-permute-start(bf16[16,1,1,1024]{3,0,2,1:T(8,128)(2,1)S(1)} %copy.28), channel_id=1, source_target_pairs={{0,30},{2,0},{4,2},{6,4},{8,6},{10,8},{12,10},{14,12},{16,14},{18,... | collective-permute-start | bytes 98312 | tf_op jit(solution)/shard_map/ppermute | solution.py:24
  157.6 8.4 %collective-permute-start.3 = (bf16[16,1,1,1024]{3,0,2,1:T(8,128)(2,1)S(1)}, bf16[16,1,1,1024]{3,0,2,1:T(8,128)(2,1)S(1)}, u32[]{:S(2)}, u32[]{:S(2)}) collective-permute-start(bf16[16,1,1,1024]{3,0,2,1:T(8,128)(2,1)S(1)} %copy.29), channel_id=1, source_target_pairs={{0,28},{2,30},{4,0},{6,2},{8,4},{10,6},{12,8},{14,10},{16,12},{18,... | collective-permute-start | bytes 98312 | tf_op jit(solution)/shard_map/ppermute | solution.py:24
  159.4 6.6 %collective-permute-start.4 = (bf16[16,1,1,1024]{3,0,2,1:T(8,128)(2,1)S(1)}, bf16[16,1,1,1024]{3,0,2,1:T(8,128)(2,1)S(1)}, u32[]{:S(2)}, u32[]{:S(2)}) collective-permute-start(bf16[16,1,1,1024]{3,0,2,1:T(8,128)(2,1)S(1)} %copy.30), channel_id=1, source_target_pairs={{0,26},{2,28},{4,30},{6,0},{8,2},{10,4},{12,6},{14,8},{16,10},{18,... | collective-permute-start | bytes 98312 | tf_op jit(solution)/shard_map/ppermute | solution.py:24
  160.1 6.8 %collective-permute-start.5 = (bf16[16,1,1,1024]{3,0,2,1:T(8,128)(2,1)S(1)}, bf16[16,1,1,1024]{3,0,2,1:T(8,128)(2,1)S(1)}, u32[]{:S(2)}, u32[]{:S(2)}) collective-permute-start(bf16[16,1,1,1024]{3,0,2,1:T(8,128)(2,1)S(1)} %copy.31), channel_id=1, source_target_pairs={{0,24},{2,26},{4,28},{6,30},{8,0},{10,2},{12,4},{14,6},{16,8},{18,... | collective-permute-start | bytes 98312 | tf_op jit(solution)/shard_map/ppermute | solution.py:24
  160.6 8.2 %collective-permute-start.6 = (bf16[16,1,1,1024]{3,0,2,1:T(8,128)(2,1)S(1)}, bf16[16,1,1,1024]{3,0,2,1:T(8,128)(2,1)S(1)}, u32[]{:S(2)}, u32[]{:S(2)}) collective-permute-start(bf16[16,1,1,1024]{3,0,2,1:T(8,128)(2,1)S(1)} %copy.32), channel_id=1, source_target_pairs={{0,22},{2,24},{4,26},{6,28},{8,30},{10,0},{12,2},{14,4},{16,6},{18... | collective-permute-start | bytes 98312 | tf_op jit(solution)/shard_map/ppermute | solution.py:24
  161.1 9.8 %collective-permute-start.7 = (bf16[16,1,1,1024]{3,0,2,1:T(8,128)(2,1)S(1)}, bf16[16,1,1,1024]{3,0,2,1:T(8,128)(2,1)S(1)}, u32[]{:S(2)}, u32[]{:S(2)}) collective-permute-start(bf16[16,1,1,1024]{3,0,2,1:T(8,128)(2,1)S(1)} %copy.33), channel_id=1, source_target_pairs={{0,20},{2,22},{4,24},{6,26},{8,28},{10,30},{12,0},{14,2},{16,4},{1... | collective-permute-start | bytes 98312 | tf_op jit(solution)/shard_map/ppermute | solution.py:24
  166.0 5.0 %collective-permute-start.8 = (bf16[16,1,1,1024]{3,0,2,1:T(8,128)(2,1)S(1)}, bf16[16,1,1,1024]{3,0,2,1:T(8,128)(2,1)S(1)}, u32[]{:S(2)}, u32[]{:S(2)}) collective-permute-start(bf16[16,1,1,1024]{3,0,2,1:T(8,128)(2,1)S(1)} %copy.34), channel_id=1, source_target_pairs={{0,18},{2,20},{4,22},{6,24},{8,26},{10,28},{12,30},{14,0},{16,2},{... | collective-permute-start | bytes 98312 | tf_op jit(solution)/shard_map/ppermute | solution.py:24
  166.1 6.9 %collective-permute-start.9 = (bf16[16,1,1,1024]{3,0,2,1:T(8,128)(2,1)S(1)}, bf16[16,1,1,1024]{3,0,2,1:T(8,128)(2,1)S(1)}, u32[]{:S(2)}, u32[]{:S(2)}) collective-permute-start(bf16[16,1,1,1024]{3,0,2,1:T(8,128)(2,1)S(1)} %copy.35), channel_id=1, source_target_pairs={{0,16},{2,18},{4,20},{6,22},{8,24},{10,26},{12,28},{14,30},{16,0},... | collective-permute-start | bytes 98312 | tf_op jit(solution)/shard_map/ppermute | solution.py:24
  166.9 8.2 %collective-permute-start.10 = (bf16[16,1,1,1024]{3,0,2,1:T(8,128)(2,1)S(1)}, bf16[16,1,1,1024]{3,0,2,1:T(8,128)(2,1)S(1)}, u32[]{:S(2)}, u32[]{:S(2)}) collective-permute-start(bf16[16,1,1,1024]{3,0,2,1:T(8,128)(2,1)S(1)} %copy.36), channel_id=1, source_target_pairs={{0,14},{2,16},{4,18},{6,20},{8,22},{10,24},{12,26},{14,28},{16,30}... | collective-permute-start | bytes 98312 | tf_op jit(solution)/shard_map/ppermute | solution.py:24
  168.8 7.8 %collective-permute-start.11 = (bf16[16,1,1,1024]{3,0,2,1:T(8,128)(2,1)S(1)}, bf16[16,1,1,1024]{3,0,2,1:T(8,128)(2,1)S(1)}, u32[]{:S(2)}, u32[]{:S(2)}) collective-permute-start(bf16[16,1,1,1024]{3,0,2,1:T(8,128)(2,1)S(1)} %copy.37), channel_id=1, source_target_pairs={{0,12},{2,14},{4,16},{6,18},{8,20},{10,22},{12,24},{14,26},{16,28}... | collective-permute-start | bytes 98312 | tf_op jit(solution)/shard_map/ppermute | solution.py:24
  170.8 5.8 %collective-permute-start.12 = (bf16[16,1,1,1024]{3,0,2,1:T(8,128)(2,1)S(1)}, bf16[16,1,1,1024]{3,0,2,1:T(8,128)(2,1)S(1)}, u32[]{:S(2)}, u32[]{:S(2)}) collective-permute-start(bf16[16,1,1,1024]{3,0,2,1:T(8,128)(2,1)S(1)} %copy.38), channel_id=1, source_target_pairs={{0,10},{2,12},{4,14},{6,16},{8,18},{10,20},{12,22},{14,24},{16,26}... | collective-permute-start | bytes 98312 | tf_op jit(solution)/shard_map/ppermute | solution.py:24
  171.1 5.7 %collective-permute-start.13 = (bf16[16,1,1,1024]{3,0,2,1:T(8,128)(2,1)S(1)}, bf16[16,1,1,1024]{3,0,2,1:T(8,128)(2,1)S(1)}, u32[]{:S(2)}, u32[]{:S(2)}) collective-permute-start(bf16[16,1,1,1024]{3,0,2,1:T(8,128)(2,1)S(1)} %copy.39), channel_id=1, source_target_pairs={{0,8},{2,10},{4,12},{6,14},{8,16},{10,18},{12,20},{14,22},{16,24},... | collective-permute-start | bytes 98312 | tf_op jit(solution)/shard_map/ppermute | solution.py:24
  173.0 5.6 %collective-permute-start.14 = (bf16[16,1,1,1024]{3,0,2,1:T(8,128)(2,1)S(1)}, bf16[16,1,1,1024]{3,0,2,1:T(8,128)(2,1)S(1)}, u32[]{:S(2)}, u32[]{:S(2)}) collective-permute-start(bf16[16,1,1,1024]{3,0,2,1:T(8,128)(2,1)S(1)} %copy.40), channel_id=1, source_target_pairs={{0,6},{2,8},{4,10},{6,12},{8,14},{10,16},{12,18},{14,20},{16,22},{... | collective-permute-start | bytes 98312 | tf_op jit(solution)/shard_map/ppermute | solution.py:24
  175.1 6.6 %collective-permute-start.15 = (bf16[16,1,1,1024]{3,0,2,1:T(8,128)(2,1)S(1)}, bf16[16,1,1,1024]{3,0,2,1:T(8,128)(2,1)S(1)}, u32[]{:S(2)}, u32[]{:S(2)}) collective-permute-start(bf16[16,1,1,1024]{3,0,2,1:T(8,128)(2,1)S(1)} %copy.41), channel_id=1, source_target_pairs={{0,4},{2,6},{4,8},{6,10},{8,12},{10,14},{12,16},{14,18},{16,20},{1... | collective-permute-start | bytes 98312 | tf_op jit(solution)/shard_map/ppermute | solution.py:24
  176.6 6.0 %collective-permute-start.16 = (bf16[16,1,1,1024]{3,0,2,1:T(8,128)(2,1)S(1)}, bf16[16,1,1,1024]{3,0,2,1:T(8,128)(2,1)S(1)}, u32[]{:S(2)}, u32[]{:S(2)}) collective-permute-start(bf16[16,1,1,1024]{3,0,2,1:T(8,128)(2,1)S(1)} %copy.42), channel_id=1, source_target_pairs={{0,2},{2,4},{4,6},{6,8},{8,10},{10,12},{12,14},{14,16},{16,18},{18... | collective-permute-start | bytes 98312 | tf_op jit(solution)/shard_map/ppermute | solution.py:24
  239.9 0.7 copy-start.1
Sparse Core Ops, SparseCore 0:
  240.8 52.9 reduce-scatter.1
